TPU v7x, 32 devices: a whole 2x2x4 slice. The times are simulated.
32 devices in a mesh: dst: 8 (over z, core), src: 4 (over y, x).
Axes of the slice: x: 2, y: 2, z: 4, core: 2. Of those that a mesh axis runs over, the one named last changes fastest.
Arguments:
- features: bfloat16 [256, 3712], P(('dst', 'src')), may hold values from -6 to 6
- edge_source: int32 [8, 2048], P('dst', 'src'), may hold values from 0 to 255, as said below
- edge_target: int32 [8, 2048], P('dst', 'src'), may hold values from 0 to 255, as said below
- edge_valid: int32 [8, 2048], P('dst', 'src'), may hold values from 0 to 1, as said below
- edge_radial: bfloat16 [8, 2048, 128], P('dst', 'src'), may hold values from -6 to 6
- edge_bias: float32 [8, 8, 2048], P('dst', None, 'src'), may hold values from -10 to 330
- w_radial: bfloat16 [128, 128], replicated, may hold values from -0.5 to 0.5
- w_zero: bfloat16 [896, 896], replicated, may hold values from -0.1875 to 0.1875
- w_one_re: bfloat16 [768, 768], replicated, may hold values from -0.15625 to 0.15625
- w_one_im: bfloat16 [768, 768], replicated, may hold values from -0.15625 to 0.15625
- w_two_re: bfloat16 [640, 640], replicated, may hold values from -0.15625 to 0.15625
- w_two_im: bfloat16 [640, 640], replicated, may hold values from -0.15625 to 0.15625
- att_vector: float32 [128], replicated, may hold values from -3 to 3
- w_out: bfloat16 [7, 128, 128], replicated, may hold values from -0.5 to 0.5
Outputs:
- attended: bfloat16 [256, 3712], P(('dst', 'src'))
Inputs may be any that keep to these rules, and one draw needn't show every extreme that they name: `edge_source`: in row d, column block s (the tile of destination block d and source block s) every entry is an atom a with (a // 8) % 4 == s. `edge_target`: in row d every entry lies in [d * 8 * 4, (d + 1) * 8 * 4); every atom is the target of at least one valid slot. `edge_valid`: about five sixteenths of the slots are valid.
All inputs are finite; a program needn't handle non-finite values.
Results may differ from a plain program's by a relative error of at most 0.0093.
Values may be sent and summed in bfloat16 or wider, within the bound.
A program may use at most 128 MiB of HBM per device.

v0:
```python
import jax
import jax.numpy as jnp
import numpy as np
from jax import lax
from jax.sharding import PartitionSpec as P

HEADS = 8
NCOEF = 29
NEG = -1e30


def merged_2(part, axis, combine):
    gathered = jax.tree.map(lambda a: lax.all_gather(a, axis), part)

    def take(source):
        return jax.tree.map(lambda a: lax.dynamic_index_in_dim(a, source, 0, False), gathered)

    return lax.fori_loop(
        1, lax.axis_size(axis), lambda source, state: combine(state, take(source)), take(0)
    )


def product(left, right):
    return jnp.dot(left, right, preferred_element_type=jnp.float32)


def exact_product(left, right):
    return jnp.dot(left, right, precision=lax.Precision.HIGHEST, preferred_element_type=jnp.float32)


def spread_heads(weights, copies, channels):
    return jnp.tile(jnp.repeat(weights, channels // weights.shape[1], axis=1), (1, copies))


def degree_table():
    return np.array(list(range(7)) + list(range(1, 7)) * 2 + list(range(2, 7)) * 2, dtype=np.int32)


def edge_messages(rows, gain, w_zero, w_one_re, w_one_im, w_two_re, w_two_im, att_vector):
    channels = gain.shape[1]
    count = rows.shape[0]

    def part(low, high):
        return (
            rows[:, low * channels : high * channels].astype(jnp.float32)
            * jnp.tile(gain, (1, high - low))
        ).astype(jnp.bfloat16)

    zero = part(0, 7)
    up_one, uq_one = (part(7, 13), part(13, 19))
    up_two, uq_two = (part(19, 24), part(24, 29))
    out_zero = product(zero, w_zero)
    yp_one = product(up_one, w_one_re) - product(uq_one, w_one_im)
    yq_one = product(up_one, w_one_im) + product(uq_one, w_one_re)
    yp_two = product(up_two, w_two_re) - product(uq_two, w_two_im)
    yq_two = product(up_two, w_two_im) + product(uq_two, w_two_re)
    active = jax.nn.silu(out_zero[:, :channels]) * att_vector[None, :]
    logit = active.reshape(count, HEADS, channels // HEADS).sum(axis=2)
    values = jnp.concatenate([out_zero, yp_one, yq_one, yp_two, yq_two], axis=1)
    return (logit, values)


def shards(
    features,
    edge_source,
    edge_target,
    edge_valid,
    edge_radial,
    edge_bias,
    w_radial,
    w_zero,
    w_one_re,
    w_one_im,
    w_two_re,
    w_two_im,
    att_vector,
    w_out,
):
    channels = w_radial.shape[1]
    own_atoms = features.shape[0]
    block_atoms = own_atoms * lax.axis_size("src")
    gathered = lax.all_gather(features, "dst", axis=0, tiled=True)
    source = edge_source[0]
    target = edge_target[0]
    valid = edge_valid[0] > 0
    slots = source.shape[0]
    local_rows = source // block_atoms * own_atoms + source % own_atoms
    rows = jnp.take(gathered, local_rows, axis=0)
    gain = product(edge_radial[0], w_radial)
    logit, values = edge_messages(
        rows, gain, w_zero, w_one_re, w_one_im, w_two_re, w_two_im, att_vector
    )
    logit = logit + edge_bias[0].T
    local_target = target - lax.axis_index("dst") * block_atoms
    member = (
        lax.broadcasted_iota(jnp.int32, (block_atoms, slots), 0) == local_target[None, :]
    ) & valid[None, :]
    one_hot = member.astype(jnp.float32)
    local_top = jnp.max(jnp.where(member[:, :, None], logit[None, :, :], NEG), axis=1)
    edge_top = exact_product(one_hot.T, local_top)
    shifted = jnp.where(valid[:, None], logit - edge_top, 0.0)
    weights = jnp.where(valid[:, None], jnp.exp(shifted), 0.0)
    weighted = values * spread_heads(weights, NCOEF, channels)
    local_den = exact_product(one_hot, weights)
    local_num = exact_product(one_hot, weighted)

    def combine_states(first, second):
        top = jnp.maximum(first[0], second[0])
        scale_first = jnp.exp(first[0] - top)
        scale_second = jnp.exp(second[0] - top)
        den = first[1] * scale_first + second[1] * scale_second
        num = first[2] * spread_heads(scale_first, NCOEF, channels) + second[2] * spread_heads(
            scale_second, NCOEF, channels
        )
        return (top, den, num)

    merged_top, merged_den, merged_num = merged_2(
        (local_top, local_den, local_num), "src", combine_states
    )
    start = lax.axis_index("src") * own_atoms
    own_den = lax.dynamic_slice_in_dim(merged_den, start, own_atoms, 0)
    own_num = lax.dynamic_slice_in_dim(merged_num, start, own_atoms, 0)
    merged = (own_num / spread_heads(own_den, NCOEF, channels)).astype(jnp.bfloat16)
    selected = w_out[degree_table()]
    projected = jnp.einsum(
        "acx,cxy->acy",
        merged.reshape(own_atoms, NCOEF, channels),
        selected,
        preferred_element_type=jnp.float32,
    )
    return projected.astype(jnp.bfloat16).reshape(own_atoms, NCOEF * channels)


def solution(mesh):
    in_specs = (
        P(("dst", "src"), None),
        P("dst", "src"),
        P("dst", "src"),
        P("dst", "src"),
        P("dst", "src", None),
        P("dst", None, "src"),
        P(),
        P(),
        P(),
        P(),
        P(),
        P(),
        P(),
        P(),
    )
    out_specs = P(("dst", "src"), None)
    return jax.shard_map(shards, mesh=mesh, in_specs=in_specs, out_specs=out_specs, check_vma=False)
```

profile of v0, /device:TPU:0, one launch (start us, length us, event | category | flops | bytes accessed | tf_op | source)
XLA Modules:
  0.0 141.0 jit_solution(15630821081774154500)
XLA Ops:
  6.5 1.2 fusion.13
  7.8 0.7 copy-done.10
  8.5 0.2 tile.103
  8.7 0.0 copy-start.16
  8.8 0.0 copy-start.18
  8.8 1.7 %copy.53 = f32[512,896]{1,0:T(8,128)} copy(f32[512,896]{0,1:T(8,128)S(1)} %bitcast.111) | data formatting | bytes 3670016 | tf_op jit(solution)/shard_map/tile | solution.py:46
  10.5 16.4 %all_gather.21 = bf16[64,3712]{1,0:T(8,128)(2,1)S(1)} all-gather(bf16[8,3712]{1,0:T(8,128)(2,1)S(1)} %copy-done.16), channel_id=1, replica_groups=mesh['dst'=8,'src'=4] {'dst'}, dimensions={0}, use_global_device_ids=true | all-gather | bytes 534528 | tf_op jit(solution)/shard_map/all_gather | solution.py:82
  27.0 4.3 %gather_fusion.1 = bf16[512,3712]{1,0:T(8,128)(2,1)} fusion(bf16[64,3712]{1,0:T(8,128)(2,1)S(1)} %all_gather.21, s32[1024]{0:T(1024)S(1)} %pad_clamp_fusion), kind=kCustom, calls=%fused_computation.1 | custom fusion | bytes 7604224 | tf_op jit(solution)/shard_map/jit(_take)/gather | solution.py:88
  31.3 2.7 %broadcast_select_fusion = bf16[512,3712]{1,0:T(8,128)(2,1)S(1)} fusion(bf16[512,3712]{1,0:T(8,128)(2,1)} %gather_fusion.1, pred[512]{0:T(512)(128)(4,1)S(1)} %compare_and_fusion), kind=kLoop, calls=%fused_computation.13 | loop fusion | flops 1900544 | bytes 7602688 | tf_op jit(solution)/shard_map/jit(_take)/select_n | solution.py:88
  34.0 0.0 copy-start.21
  34.0 0.0 copy-start.19
  34.0 0.0 copy-start.20
  34.0 2.5 %constant_dynamic-update-slice_fusion = (f32[512,3712]{1,0:T(8,128)}, f32[512,896]{1,0:T(8,128)S(1)}) fusion(bf16[896,896]{1,0:T(8,128)(2,1)S(1)} %copy-done, f32[512,896]{1,0:T(8,128)S(1)} %copy-done.5, bf16[512,3712]{1,0:T(8,128)(2,1)S(1)} %broadcast_select_fusion), kind=kOutput, calls=%fused_computation.46 | convolution fusion | flops 823459840 | bytes 8028160 | tf_op jit(solution)/shard_map/dot_general | solution.py:24
  36.5 0.1 multiply_multiply_fusion
  36.6 0.1 copy.54
  36.9 0.2 select_reduce_fusion
  37.1 0.2 fusion.10
  37.3 0.2 copy-done.11
  37.5 1.4 tile.105
  38.8 1.9 %copy.57 = f32[512,768]{1,0:T(8,128)S(1)} copy(f32[512,768]{0,1:T(8,128)} %bitcast.114) | data formatting | bytes 3145728 | tf_op jit(solution)/shard_map/tile | solution.py:46
  40.7 3.6 %fusion.32 = f32[512,768]{1,0:T(8,128)} fusion(bf16[768,768]{1,0:T(8,128)(2,1)} %param.26, f32[512,768]{1,0:T(8,128)S(1)} %copy.57, bf16[512,3712]{1,0:T(8,128)(2,1)} %copy-done.3), kind=kOutput, calls=%fused_computation.80 | convolution fusion | flops 605159424 | bytes 5111808 | tf_op jit(solution)/shard_map/dot_general | solution.py:24
  44.4 3.1 %fusion.31 = f32[512,768]{1,0:T(8,128)} fusion(bf16[768,768]{1,0:T(8,128)(2,1)S(1)} %copy-done.9, f32[512,768]{1,0:T(8,128)S(1)} %copy.57, bf16[512,3712]{1,0:T(8,128)(2,1)} %copy-done.3), kind=kOutput, calls=%fused_computation.79 | convolution fusion | flops 605159424 | bytes 5111808 | tf_op jit(solution)/shard_map/dot_general | solution.py:24
  47.4 1.2 tile.107
  48.7 2.8 %copy.60 = f32[512,640]{1,0:T(8,128)} copy(f32[512,640]{0,1:T(8,128)} %bitcast.115) | data formatting | bytes 2621440 | tf_op jit(solution)/shard_map/tile | solution.py:46
  51.5 3.7 %fusion.30 = f32[512,640]{1,0:T(8,128)} fusion(bf16[640,640]{1,0:T(8,128)(2,1)} %param.28, f32[512,640]{1,0:T(8,128)} %copy.60, bf16[512,3712]{1,0:T(8,128)(2,1)} %copy-done.3), kind=kOutput, calls=%fused_computation.78 | convolution fusion | flops 420413440 | bytes 4096000 | tf_op jit(solution)/shard_map/dot_general | solution.py:24
  55.2 2.9 %fusion.29 = f32[512,640]{1,0:T(8,128)} fusion(bf16[640,640]{1,0:T(8,128)(2,1)S(1)} %copy-done.13, f32[512,640]{1,0:T(8,128)S(1)} %copy-done.1, bf16[512,3712]{1,0:T(8,128)(2,1)} %copy-done.3), kind=kOutput, calls=%fused_computation.77 | convolution fusion | flops 420413440 | bytes 4096000 | tf_op jit(solution)/shard_map/dot_general | solution.py:24
  58.1 4.0 %tile.110 = f32[512,29,128]{0,2,1:T(8,128)} broadcast(f32[512,128]{0,1:T(8,128)S(1)} %bitcast.117), dimensions={0,2} | broadcast | bytes 7864320 | tf_op jit(solution)/shard_map/tile | solution.py:32
  62.2 8.8 %copy.62 = f32[512,3712]{1,0:T(8,128)} copy(f32[512,3712]{0,1:T(8,128)} %bitcast.110) | data formatting | bytes 15204352 | tf_op jit(solution)/shard_map/tile | solution.py:32
  71.0 4.1 %subtract_dynamic-update-slice_fusion = f32[512,3712]{1,0:T(8,128)} fusion(f32[512,3712]{1,0:T(8,128)} %get-tuple-element.202, f32[512,768]{1,0:T(8,128)} %fusion.32, bf16[768,768]{1,0:T(8,128)(2,1)} %param.27, f32[512,768]{1,0:T(8,128)S(1)} %copy.57, bf16[512,3712]{1,0:T(8,128)(2,1)} %copy-done.3), kind=kOutput, calls=%fused_computation.16 | convolution fusion | flops 605552640 | bytes 6684672 | tf_op jit(solution)/shard_map/dot_general | solution.py:24
  75.2 0.0 copy-start.15
  75.2 3.5 %add_dynamic-update-slice_fusion = f32[512,3712]{1,0:T(8,128)} fusion(f32[512,3712]{1,0:T(8,128)} %subtract_dynamic-update-slice_fusion, f32[512,768]{1,0:T(8,128)S(1)} %copy-done.6, bf16[768,768]{1,0:T(8,128)(2,1)} %param.26, f32[512,768]{1,0:T(8,128)S(1)} %copy.57, bf16[512,3712]{1,0:T(8,128)(2,1)S(1)} %copy-done.4), kind=kOutput, calls=%fused_computation.15 | convolution fusion | flops 605552640 | bytes 6684672 | tf_op jit(solution)/shard_map/dot_general | solution.py:24
  78.7 1.9 %fusion.6 = f32[512,3712]{1,0:T(8,128)} fusion(f32[512,3712]{1,0:T(8,128)} %add_dynamic-update-slice_fusion, f32[512,640]{1,0:T(8,128)S(1)} %copy-done.8, bf16[640,640]{1,0:T(8,128)(2,1)S(1)} %copy-done.14, f32[512,640]{1,0:T(8,128)S(1)} %copy-done.2, bf16[512,3712]{1,0:T(8,128)(2,1)S(1)} %copy-done.4), kind=kOutput, calls=%fused_computation.22 | convolution fusion | flops 420741120 | bytes 5406720 | tf_op jit(solution)/shard_map/dot_general | solution.py:24
  80.6 1.9 %fusion.5 = f32[512,3712]{1,0:T(8,128)} fusion(f32[512,3712]{1,0:T(8,128)} %fusion.6, f32[512,640]{1,0:T(8,128)S(1)} %copy-done.7, bf16[640,640]{1,0:T(8,128)(2,1)S(1)} %copy-done.15, f32[512,640]{1,0:T(8,128)S(1)} %copy-done.2, bf16[512,3712]{1,0:T(8,128)(2,1)S(1)} %copy-done.4), kind=kOutput, calls=%fused_computation.20 | convolution fusion | flops 420741120 | bytes 5406720 | tf_op jit(solution)/shard_map/dot_general | solution.py:24
  82.5 0.0 copy-start.12
  82.6 7.2 %fusion.3 = f32[32,3712]{1,0:T(8,128)} fusion(f32[512,3712]{1,0:T(8,128)} %fusion.5, f32[512,3712]{1,0:T(8,128)S(1)} %bitcast.109, s32[512]{0:T(512)S(1)} %bitcast.121, pred[512]{0:T(512)(128)(4,1)S(1)} %compare_reduce_fusion), kind=kOutput, calls=%fused_computation.11 | convolution fusion | flops 731742208 | bytes 15682048 | tf_op jit(solution)/shard_map/dot_general | solution.py:28
  89.8 0.0 all-gather.7.cloned.1.call-update
  89.8 0.1 copy.55
  89.9 1.6 %gather_fusion = bf16[29,128,128]{2,1,0:T(8,128)(2,1)} fusion(bf16[7,128,128]{2,1,0:T(8,128)(2,1)S(1)} %copy-done.12, s32[1024]{0:T(1024)S(1)} %pad_clamp_fusion.1), kind=kCustom, calls=%fused_computation | custom fusion | bytes 1900660 | tf_op jit(solution)/shard_map/gather | solution.py:124
  91.5 8.2 %all-gather.3 = f32[4,32,8]{1,2,0:T(8,128)S(1)} all-gather(f32[1,32,8]{1,2,0:T(8,128)S(1)} %copy.55), channel_id=2, replica_groups=mesh['dst'=8,'src'=4] {'src'}, dimensions={0}, use_global_device_ids=true | all-gather | bytes 5120 | tf_op jit(solution)/shard_map/all_gather | solution.py:13
  99.7 0.1 convolution_bitcast_fusion
  99.8 8.4 %all-gather.4 = f32[4,32,8]{1,2,0:T(8,128)S(1)} all-gather(f32[1,32,8]{1,2,0:T(8,128)S(1)} %convolution_bitcast_fusion), channel_id=3, replica_groups=mesh['dst'=8,'src'=4] {'src'}, dimensions={0}, use_global_device_ids=true | all-gather | bytes 5120 | tf_op jit(solution)/shard_map/all_gather | solution.py:13
  108.2 16.4 %all-gather.7.cloned.1.call-done = f32[128,3712]{1,0:T(8,128)} async-done(((f32[32,3712]{1,0:T(8,128)}), f32[128,3712]{1,0:T(8,128)}) %all-gather.7.cloned.1.call-update) | async-done | bytes 1900560 | tf_op jit(solution)/shard_map/all_gather | solution.py:13
  124.7 1.1 slice.44
  125.7 5.9 %while.19 = (s32[]{:T(128)}, f32[32,8]{0,1:T(8,128)S(1)}, f32[32,8]{0,1:T(8,128)S(1)}, f32[32,3712]{1,0:T(8,128)S(1)}, f32[4,32,8]{1,2,0:T(8,128)S(1)}, /*index=...) while((s32[]{:T(128)}, f32[32,8]{0,1:T(8,128)S(1)}, ...), condition=%wide.region_3.4_spmd, body=%wide.region_2.3_spmd.sunk | while | flops 357893 | bytes 3467415 | solution.py:18
  125.8 0.1 copy.75
  125.8 0.1 tile.121
  125.9 0.1 copy.76
  126.0 0.1 tile.122
  126.0 1.7 %fusion.50 = f32[32,3712]{1,0:T(8,128)S(1)} fusion(f32[4,8,29,128]{3,2,1,0:T(8,128)S(1)} %bitcast.106, f32[32,3712]{1,0:T(8,128)S(1)} %get-tuple-element.268, f32[4,8,29,128]{3,2,1,0:T(8,128)S(1)} %bitcast.107, f32[4,32,3712]{2,1,0:T(8,128)} %get-tuple-element.281, s32[]{:T(128)S(6)} %select_n.137), kind=kLoop, calls=%fused_computation.3.clone.1 | loop fusion | flops 356352 | bytes 2375684 | tf_op jit(solution)/shard_map/while/body/eval_jaxpr/add | solution.py:112
  127.8 0.1 copy.75
  127.8 0.1 tile.121
  127.9 0.1 copy.76
  127.9 0.1 tile.122
  128.0 1.7 %fusion.50 = f32[32,3712]{1,0:T(8,128)S(1)} fusion(f32[4,8,29,128]{3,2,1,0:T(8,128)S(1)} %bitcast.106, f32[32,3712]{1,0:T(8,128)S(1)} %get-tuple-element.268, f32[4,8,29,128]{3,2,1,0:T(8,128)S(1)} %bitcast.107, f32[4,32,3712]{2,1,0:T(8,128)} %get-tuple-element.281, s32[]{:T(128)S(6)} %select_n.137), kind=kLoop, calls=%fused_computation.3.clone.1 | loop fusion | flops 356352 | bytes 2375684 | tf_op jit(solution)/shard_map/while/body/eval_jaxpr/add | solution.py:112
  129.7 0.1 copy.75
  129.8 0.1 tile.121
  129.9 0.1 copy.76
  129.9 0.1 tile.122
  130.0 1.7 %fusion.50 = f32[32,3712]{1,0:T(8,128)S(1)} fusion(f32[4,8,29,128]{3,2,1,0:T(8,128)S(1)} %bitcast.106, f32[32,3712]{1,0:T(8,128)S(1)} %get-tuple-element.268, f32[4,8,29,128]{3,2,1,0:T(8,128)S(1)} %bitcast.107, f32[4,32,3712]{2,1,0:T(8,128)} %get-tuple-element.281, s32[]{:T(128)S(6)} %select_n.137), kind=kLoop, calls=%fused_computation.3.clone.1 | loop fusion | flops 356352 | bytes 2375684 | tf_op jit(solution)/shard_map/while/body/eval_jaxpr/add | solution.py:112
  131.7 0.1 constant_dynamic-slice_fusion
  131.7 0.1 copy.63
  131.8 0.1 broadcast_in_dim.91
  131.9 0.1 tile.112
  132.0 2.2 %fusion.7 = bf16[8,3712]{1,0:T(8,128)(2,1)} fusion(bf16[29,128,128]{2,1,0:T(8,128)(2,1)} %gather_fusion, f32[32,3712]{1,0:T(8,128)S(1)} %get-tuple-element.182, s32[]{:T(128)S(6)} %select_n.99, f32[8,128]{1,0:T(8,128)S(1)} %tile.112), kind=kOutput, calls=%fused_computation.26 | convolution fusion | flops 7691264 | bytes 1132548 | tf_op jit(solution)/shard_map/acx,cxy->acy/dot_general | solution.py:125
  (64 shorter events, 0.3 us)
Async XLA Ops:
  6.5 27.4 %copy-start = (bf16[896,896]{1,0:T(8,128)(2,1)S(1)}, bf16[896,896]{1,0:T(8,128)(2,1)}, u32[]{:S(2)}) copy-start(bf16[896,896]{1,0:T(8,128)(2,1)} %param.25) | copy-start | bytes 4816900
  6.5 118.1 %all-gather.7.cloned.1.call-start = ((), (), s32[]{:S(2)}) async-start(), calls=%async_computation | async-start | bytes 2375680 | tf_op jit(solution)/shard_map/all_gather | solution.py:13
  7.8 0.7 copy-start.10
  8.7 1.7 %copy-start.16 = (bf16[8,3712]{1,0:T(8,128)(2,1)S(1)}, bf16[8,3712]{1,0:T(8,128)(2,1)}, u32[]{:S(2)}) copy-start(bf16[8,3712]{1,0:T(8,128)(2,1)} %param.18) | copy-start | bytes 178180
  8.8 18.1 %copy-start.18 = (s32[1,512]{1,0:T(1,128)S(1)}, s32[1,512]{1,0:T(1,128)}, u32[]{:S(2)}) copy-start(s32[1,512]{1,0:T(1,128)} %param.19) | copy-start | bytes 6148
  31.3 2.7 %copy-start.5 = (f32[512,896]{1,0:T(8,128)S(1)}, f32[512,896]{1,0:T(8,128)}, u32[]{:S(2)}) copy-start(f32[512,896]{1,0:T(8,128)} %copy.53) | copy-start | bytes 5505028
  34.0 2.6 %copy-start.3 = (bf16[512,3712]{1,0:T(8,128)(2,1)}, bf16[512,3712]{1,0:T(8,128)(2,1)S(1)}, u32[]{:S(2)}) copy-start(bf16[512,3712]{1,0:T(8,128)(2,1)S(1)} %broadcast_select_fusion) | copy-start | bytes 11403268
  34.0 2.6 %copy-start.21 = (f32[128]{0:T(128)S(1)}, f32[128]{0:T(128)}, u32[]{:S(2)}) copy-start(f32[128]{0:T(128)} %param.30) | copy-start | bytes 1540
  34.0 2.8 %copy-start.19 = (s32[1,512]{1,0:T(1,128)S(1)}, s32[1,512]{1,0:T(1,128)}, u32[]{:S(2)}) copy-start(s32[1,512]{1,0:T(1,128)} %param.21) | copy-start | bytes 6148
  34.0 2.8 %copy-start.17 = (f32[1,8,512]{2,1,0:T(8,128)S(1)}, f32[1,8,512]{2,1,0:T(8,128)}, u32[]{:S(2)}) copy-start(f32[1,8,512]{2,1,0:T(8,128)} %param.23) | copy-start | bytes 49156
  34.0 2.9 %copy-start.20 = (s32[1,512]{1,0:T(1,128)S(1)}, s32[1,512]{1,0:T(1,128)}, u32[]{:S(2)}) copy-start(s32[1,512]{1,0:T(1,128)} %param.20) | copy-start | bytes 6148
  36.5 1.0 copy-start.11
  40.7 3.7 %copy-start.9 = (bf16[768,768]{1,0:T(8,128)(2,1)S(1)}, bf16[768,768]{1,0:T(8,128)(2,1)}, u32[]{:S(2)}) copy-start(bf16[768,768]{1,0:T(8,128)(2,1)} %param.27) | copy-start | bytes 3538948
  51.4 3.7 %copy-start.1 = (f32[512,640]{1,0:T(8,128)S(1)}, f32[512,640]{1,0:T(8,128)}, u32[]{:S(2)}) copy-start(f32[512,640]{1,0:T(8,128)} %copy.60) | copy-start | bytes 3932164
  51.4 3.7 %copy-start.13 = (bf16[640,640]{1,0:T(8,128)(2,1)S(1)}, bf16[640,640]{1,0:T(8,128)(2,1)}, u32[]{:S(2)}) copy-start(bf16[640,640]{1,0:T(8,128)(2,1)} %param.29) | copy-start | bytes 2457604
  71.0 4.2 %copy-start.4 = (bf16[512,3712]{1,0:T(8,128)(2,1)S(1)}, bf16[512,3712]{1,0:T(8,128)(2,1)}, u32[]{:S(2)}) copy-start(bf16[512,3712]{1,0:T(8,128)(2,1)} %copy-done.3) | copy-start | bytes 11403268
  71.0 4.2 %copy-start.6 = (f32[512,768]{1,0:T(8,128)S(1)}, f32[512,768]{1,0:T(8,128)}, u32[]{:S(2)}) copy-start(f32[512,768]{1,0:T(8,128)} %fusion.31) | copy-start | bytes 4718596
  71.0 7.7 %copy-start.8 = (f32[512,640]{1,0:T(8,128)S(1)}, f32[512,640]{1,0:T(8,128)}, u32[]{:S(2)}) copy-start(f32[512,640]{1,0:T(8,128)} %fusion.30) | copy-start | bytes 3932164
  75.1 3.5 %copy-start.2 = (f32[512,640]{1,0:T(8,128)S(1)}, f32[512,640]{1,0:T(8,128)}, u32[]{:S(2)}) copy-start(f32[512,640]{1,0:T(8,128)} %copy.60) | copy-start | bytes 3932164
  75.2 3.5 %copy-start.14 = (bf16[640,640]{1,0:T(8,128)(2,1)S(1)}, bf16[640,640]{1,0:T(8,128)(2,1)}, u32[]{:S(2)}) copy-start(bf16[640,640]{1,0:T(8,128)(2,1)} %param.29) | copy-start | bytes 2457604
  75.2 5.4 %copy-start.15 = (bf16[640,640]{1,0:T(8,128)(2,1)S(1)}, bf16[640,640]{1,0:T(8,128)(2,1)}, u32[]{:S(2)}) copy-start(bf16[640,640]{1,0:T(8,128)(2,1)} %param.28) | copy-start | bytes 2457604
  75.2 7.4 %slice-start = ((s8[7602176]{0:T(1024)(128)(4,1)}), s8[4194304]{0:T(1024)(128)(4,1)S(1)}, s32[]{:S(2)}) async-start(s8[7602176]{0:T(1024)(128)(4,1)} %bitcast.108), calls=%async_computation.1 | async-start | bytes 8388608
  78.7 1.9 %copy-start.7 = (f32[512,640]{1,0:T(8,128)S(1)}, f32[512,640]{1,0:T(8,128)}, u32[]{:S(2)}) copy-start(f32[512,640]{1,0:T(8,128)} %fusion.29) | copy-start | bytes 3932164
  78.7 3.8 %slice-start.1 = ((s8[7602176]{0:T(1024)(128)(4,1)}), s8[3407872]{0:T(1024)(128)(4,1)S(1)}, s32[]{:S(2)}) async-start(s8[7602176]{0:T(1024)(128)(4,1)} %bitcast.108), calls=%async_computation.2 | async-start | bytes 6815744
  82.5 7.3 %copy-start.22 = (s32[29]{0:T(128)S(1)}, s32[29]{0:T(128)}, u32[]{:S(2)}) copy-start(s32[29]{0:T(128)} %constant.134) | copy-start | bytes 352
  82.5 7.3 %copy-start.12 = (bf16[7,128,128]{2,1,0:T(8,128)(2,1)S(1)}, bf16[7,128,128]{2,1,0:T(8,128)(2,1)}, u32[]{:S(2)}) copy-start(bf16[7,128,128]{2,1,0:T(8,128)(2,1)} %param.31) | copy-start | bytes 688132
Sparse Core Ops, SparseCore 0:
  89.9 34.7 all-gather.6
where the time goes:
time: 142 us; the launch traced here: 141 us
  matrix products  38.3 us (27%)
  blocking collectives  33 us (23%)
  local copies, waits for them, and re-layouts  31.2 us (22%)
  waiting for transfers between devices  16.5 us (12%)
  between operations  13.7 us (10%)
  other arithmetic  8.12 us (6%)
    dot_general x10, matrix products, product(): return jnp.dot(left, right, preferred_element_type=jnp.float32)  28.6 us
    all_gather x2, blocking collectives, merged_2(): gathered = jax.tree.map(lambda a: lax.all_gather(a, axis), part)  16.6 us
    all_gather x1, waiting for transfers between devices, merged_2(): gathered = jax.tree.map(lambda a: lax.all_gather(a, axis), part)  16.4 us
    all_gather x1, blocking collectives, shards(): gathered = lax.all_gather(features, 'dst', axis=0, tiled=True)  16.4 us
    another operation x15, local copies, waits for them, and re-layouts, spread_heads(): jnp.tile(jnp.repeat(weights, channels // weights.shape[1], axis=1), (1, c...  13.6 us
    another operation x6, local copies, waits for them, and re-layouts, part(): jnp.tile(gain, (1, high - low))  9.16 us
    dot_general x3, matrix products, exact_product(): jnp.dot(left, right, precision=lax.Precision.HIGHEST, preferred_element_t...  7.55 us
    add x3, other arithmetic, combine_states(): first[2] * spread_heads(scale_first, NCOEF, channels)  5.02 us
  transfers between devices with their start and end apart: 1, of which 1 were waited for; matrix products, arithmetic and copies ran while one was open for 1% of the time, Pallas kernels for 0%

commit v1 on v0

--- a/solution.py
+++ b/solution.py
@@ -7,6 +7,23 @@
 HEADS = 8
 NCOEF = 29
 NEG = -1e30
+
+
+def joined_along(blocks, dim):
+    lengths = list(blocks.shape[1:])
+    lengths[dim] *= blocks.shape[0]
+    return jnp.moveaxis(blocks, 0, dim).reshape(lengths)
+
+
+def collected_by_bits(value, axis):
+    length, index = (lax.axis_size(axis), lax.axis_index(axis))
+    blocks, distance = (value[None], 1)
+    while distance < length:
+        theirs = lax.ppermute(blocks, axis, [(i, i ^ distance) for i in range(length)])
+        low = index & distance == 0
+        blocks = jnp.concatenate([jnp.where(low, blocks, theirs), jnp.where(low, theirs, blocks)])
+        distance *= 2
+    return blocks
 
 
 def merged_2(part, axis, combine):
@@ -79,7 +96,7 @@
     channels = w_radial.shape[1]
     own_atoms = features.shape[0]
     block_atoms = own_atoms * lax.axis_size("src")
-    gathered = lax.all_gather(features, "dst", axis=0, tiled=True)
+    gathered = joined_along(collected_by_bits(features, "dst"), 0)
     source = edge_source[0]
     target = edge_target[0]
     valid = edge_valid[0] > 0

time: 142 us -> 138 us (0.972)
  blocking collectives: 33 us -> 16.4 us
  other arithmetic: 8.12 us -> 14.5 us
  waiting for transfers between devices: 16.5 us -> 22.7 us
  starting transfers between devices: 0.01 us -> 6 us
  matrix products: 38.3 us -> 34.8 us
  local copies, waits for them, and re-layouts: 31.2 us -> 29.1 us
    all_gather x1 -> x0, blocking collectives: 16.4 us -> none  [shards(): gathered = lax.all_gather(features, 'dst', axis=0, tiled=True)]
    ppermute x0 -> x3, waiting for transfers between devices: none -> 6.07 us  [collected_by_bits(): lax.ppermute(blocks, axis, [(i, i ^ distance) for i in range(length)])]
    ppermute x0 -> x3, starting transfers between devices: none -> 5.99 us  [collected_by_bits(): lax.ppermute(blocks, axis, [(i, i ^ distance) for i in range(length)])]
    dot_general x10, matrix products: 28.6 us -> 25 us  [product(): return jnp.dot(left, right, preferred_element_type=jnp.float32)]
    another operation x6, local copies, waits for them, and re-layouts: 9.16 us -> 7.27 us  [part(): jnp.tile(gain, (1, high - low))]
    select_n x0 -> x3, other arithmetic: none -> 1.87 us  [collected_by_bits(): jnp.where(low, blocks, theirs)]
  transfers between devices with their start and end apart: 1 -> 4, of which waited for: 1 -> 3; matrix products, arithmetic and copies ran while one was open for 1% -> 10% of each run, Pallas kernels for 0% -> 0%
where the time goes in v1:
time: 138 us; the launch traced here: 137 us
  matrix products  34.8 us (25%)
  local copies, waits for them, and re-layouts  29.1 us (21%)
  waiting for transfers between devices  22.7 us (16%)
  blocking collectives  16.4 us (12%)
  other arithmetic  14.5 us (11%)
  between operations  13.7 us (10%)
  starting transfers between devices  6 us (4%)
    dot_general x10, matrix products, product(): return jnp.dot(left, right, preferred_element_type=jnp.float32)  25 us
    all_gather x1, waiting for transfers between devices, merged_2(): gathered = jax.tree.map(lambda a: lax.all_gather(a, axis), part)  16.6 us
    all_gather x2, blocking collectives, merged_2(): gathered = jax.tree.map(lambda a: lax.all_gather(a, axis), part)  16.4 us
    another operation x15, local copies, waits for them, and re-layouts, spread_heads(): jnp.tile(jnp.repeat(weights, channels // weights.shape[1], axis=1), (1, c...  13.5 us
    dot_general x3, matrix products, exact_product(): jnp.dot(left, right, precision=lax.Precision.HIGHEST, preferred_element_t...  7.58 us
    another operation x6, local copies, waits for them, and re-layouts, part(): jnp.tile(gain, (1, high - low))  7.27 us
    ppermute x3, waiting for transfers between devices, collected_by_bits(): lax.ppermute(blocks, axis, [(i, i ^ distance) for i in range(length)])  6.07 us
    ppermute x3, starting transfers between devices, collected_by_bits(): lax.ppermute(blocks, axis, [(i, i ^ distance) for i in range(length)])  5.99 us
  transfers between devices with their start and end apart: 4, of which 3 were waited for; matrix products, arithmetic and copies ran while one was open for 10% of the time, Pallas kernels for 0%

profile of v1, /device:TPU:0, one launch (start us, length us, event | category | flops | bytes accessed | tf_op | source)
XLA Modules:
  0.0 137.4 jit_solution(14938162441934703827)
XLA Ops:
  6.5 0.5 collective-permute-start
  7.0 0.7 compare_select_fusion
  7.7 1.8 %fusion.13 = f32[512,128]{0,1:T(8,128)} fusion(bf16[128,128]{1,0:T(8,128)(2,1)} %param.24, bf16[1,512,128]{2,1,0:T(8,128)(2,1)} %param.22), kind=kOutput, calls=%fused_computation.41 | convolution fusion | flops 16777216 | bytes 425984 | tf_op jit(solution)/shard_map/dot_general | solution.py:41
  9.6 0.7 broadcast_subtract_fusion
  10.3 0.8 broadcast_select_fusion.6
  11.1 2.7 %collective-permute-start.1 = (bf16[2,8,3712]{2,1,0:T(8,128)(2,1)S(1)}, bf16[2,8,3712]{2,1,0:T(8,128)(2,1)S(1)}, u32[]{:S(2)}, u32[]{:S(2)}) collective-permute-start(bf16[2,8,3712]{2,1,0:T(8,128)(2,1)S(1)} %pad_maximum_fusion.1), channel_id=1, source_target_pairs={{0,8},{4,12},{8,0},{12,4},{16,24},{20,28},{24,16},{28,20},{1,9},{5... | collective-permute-start | bytes 356360 | tf_op jit(solution)/shard_map/ppermute | solution.py:22
  13.9 0.7 compare_and_fusion
  14.6 0.7 compare_reduce_fusion
  15.3 2.4 %collective-permute-done.1 = bf16[2,8,3712]{2,1,0:T(8,128)(2,1)S(1)} collective-permute-done((bf16[2,8,3712]{2,1,0:T(8,128)(2,1)S(1)}, bf16[2,8,3712]{2,1,0:T(8,128)(2,1)S(1)}, u32[]{:S(2)}, u32[]{:S(2)}) %collective-permute-start.1) | collective-permute-done | bytes 118816 | tf_op jit(solution)/shard_map/ppermute | solution.py:22
  17.7 0.8 pad_maximum_fusion
  18.5 2.8 %collective-permute-start.2 = (bf16[4,8,3712]{2,1,0:T(8,128)(2,1)}, bf16[4,8,3712]{2,1,0:T(8,128)(2,1)}, u32[]{:S(2)}, u32[]{:S(2)}) collective-permute-start(bf16[4,8,3712]{2,1,0:T(8,128)(2,1)} %pad_maximum_fusion), channel_id=1, source_target_pairs={{0,16},{4,20},{8,24},{12,28},{16,0},{20,4},{24,8},{28,12},{1,17},{... | collective-permute-start | bytes 712712 | tf_op jit(solution)/shard_map/ppermute | solution.py:22
  21.3 1.2 tile.103
  22.4 1.7 %copy.53 = f32[512,896]{1,0:T(8,128)} copy(f32[512,896]{0,1:T(8,128)S(1)} %bitcast.116) | data formatting | bytes 3670016 | tf_op jit(solution)/shard_map/tile | solution.py:63
  24.2 1.1 tile.105
  25.3 1.6 %copy.57 = f32[512,768]{1,0:T(8,128)} copy(f32[512,768]{0,1:T(8,128)S(1)} %bitcast.119) | data formatting | bytes 3145728 | tf_op jit(solution)/shard_map/tile | solution.py:63
  26.9 0.2 tile.107
  27.1 1.5 %copy.60 = f32[512,640]{1,0:T(8,128)} copy(f32[512,640]{0,1:T(8,128)S(1)} %bitcast.120) | data formatting | bytes 2621440 | tf_op jit(solution)/shard_map/tile | solution.py:63
  28.6 3.7 %collective-permute-done.2 = bf16[4,8,3712]{2,1,0:T(8,128)(2,1)} collective-permute-done((bf16[4,8,3712]{2,1,0:T(8,128)(2,1)}, bf16[4,8,3712]{2,1,0:T(8,128)(2,1)}, u32[]{:S(2)}, u32[]{:S(2)}) %collective-permute-start.2) | collective-permute-done | bytes 237600 | tf_op jit(solution)/shard_map/ppermute | solution.py:22
  32.3 1.0 broadcast_select_fusion.2
  33.3 0.1 maximum_bitcast_fusion
  33.4 4.3 %gather_fusion.1 = bf16[512,3712]{1,0:T(8,128)(2,1)} fusion(bf16[64,3712]{1,0:T(8,128)(2,1)S(1)} %maximum_bitcast_fusion, s32[1024]{0:T(1024)S(1)} %pad_clamp_fusion), kind=kCustom, calls=%fused_computation.1 | custom fusion | bytes 7604224 | tf_op jit(solution)/shard_map/jit(_take)/gather | solution.py:105
  37.7 2.7 %broadcast_select_fusion = bf16[512,3712]{1,0:T(8,128)(2,1)S(1)} fusion(bf16[512,3712]{1,0:T(8,128)(2,1)} %gather_fusion.1, pred[512]{0:T(512)(128)(4,1)S(1)} %compare_and_fusion), kind=kLoop, calls=%fused_computation.13 | loop fusion | flops 1900544 | bytes 7602688 | tf_op jit(solution)/shard_map/jit(_take)/select_n | solution.py:105
  40.4 2.5 %constant_dynamic-update-slice_fusion = (f32[512,3712]{1,0:T(8,128)}, f32[512,896]{1,0:T(8,128)S(1)}) fusion(bf16[896,896]{1,0:T(8,128)(2,1)S(1)} %copy-done, f32[512,896]{1,0:T(8,128)S(1)} %copy-done.7, bf16[512,3712]{1,0:T(8,128)(2,1)S(1)} %broadcast_select_fusion), kind=kOutput, calls=%fused_computation.55 | convolution fusion | flops 823459840 | bytes 8028160 | tf_op jit(solution)/shard_map/dot_general | solution.py:41
  42.9 0.1 multiply_multiply_fusion
  43.0 0.8 copy.54
  43.8 1.0 bitcast_reduce_fusion
  44.8 0.2 select_reduce_fusion
  45.0 0.2 fusion.10
  45.2 3.7 %fusion.32 = f32[512,768]{1,0:T(8,128)} fusion(bf16[768,768]{1,0:T(8,128)(2,1)} %param.26, f32[512,768]{1,0:T(8,128)S(1)} %copy-done.1, bf16[512,3712]{1,0:T(8,128)(2,1)} %copy-done.4), kind=kOutput, calls=%fused_computation.89 | convolution fusion | flops 605159424 | bytes 5111808 | tf_op jit(solution)/shard_map/dot_general | solution.py:41
  48.9 1.9 %fusion.31 = f32[512,768]{1,0:T(8,128)} fusion(bf16[768,768]{1,0:T(8,128)(2,1)S(1)} %copy-done.11, f32[512,768]{1,0:T(8,128)S(1)} %copy-done.1, bf16[512,3712]{1,0:T(8,128)(2,1)S(1)} %copy-done.5), kind=kOutput, calls=%fused_computation.88 | convolution fusion | flops 605159424 | bytes 5111808 | tf_op jit(solution)/shard_map/dot_general | solution.py:41
  50.9 1.8 %fusion.30 = f32[512,640]{1,0:T(8,128)} fusion(bf16[640,640]{1,0:T(8,128)(2,1)S(1)} %copy-done.16, f32[512,640]{1,0:T(8,128)S(1)} %copy-done.2, bf16[512,3712]{1,0:T(8,128)(2,1)S(1)} %copy-done.5), kind=kOutput, calls=%fused_computation.87 | convolution fusion | flops 420413440 | bytes 4096000 | tf_op jit(solution)/shard_map/dot_general | solution.py:41
  52.8 1.8 %fusion.29 = f32[512,640]{1,0:T(8,128)} fusion(bf16[640,640]{1,0:T(8,128)(2,1)S(1)} %copy-done.14, f32[512,640]{1,0:T(8,128)S(1)} %copy-done.2, bf16[512,3712]{1,0:T(8,128)(2,1)S(1)} %copy-done.5), kind=kOutput, calls=%fused_computation.86 | convolution fusion | flops 420413440 | bytes 4096000 | tf_op jit(solution)/shard_map/dot_general | solution.py:41
  54.6 4.0 %tile.110 = f32[512,29,128]{0,2,1:T(8,128)} broadcast(f32[512,128]{0,1:T(8,128)S(1)} %bitcast.122), dimensions={0,2} | broadcast | bytes 7864320 | tf_op jit(solution)/shard_map/tile | solution.py:49
  58.6 8.8 %copy.62 = f32[512,3712]{1,0:T(8,128)} copy(f32[512,3712]{0,1:T(8,128)} %bitcast.115) | data formatting | bytes 15204352 | tf_op jit(solution)/shard_map/tile | solution.py:49
  67.4 4.1 %subtract_dynamic-update-slice_fusion = f32[512,3712]{1,0:T(8,128)} fusion(f32[512,3712]{1,0:T(8,128)} %get-tuple-element.208, f32[512,768]{1,0:T(8,128)} %fusion.32, bf16[768,768]{1,0:T(8,128)(2,1)} %param.27, f32[512,768]{1,0:T(8,128)S(1)} %copy-done.1, bf16[512,3712]{1,0:T(8,128)(2,1)} %copy-done.4), kind=kOutput, calls=%fused_computation.16 | convolution fusion | flops 605552640 | bytes 6684672 | tf_op jit(solution)/shard_map/dot_general | solution.py:41
  71.6 3.4 %add_dynamic-update-slice_fusion = f32[512,3712]{1,0:T(8,128)} fusion(f32[512,3712]{1,0:T(8,128)} %subtract_dynamic-update-slice_fusion, f32[512,768]{1,0:T(8,128)S(1)} %copy-done.8, bf16[768,768]{1,0:T(8,128)(2,1)} %param.26, f32[512,768]{1,0:T(8,128)S(1)} %copy-done.1, bf16[512,3712]{1,0:T(8,128)(2,1)S(1)} %copy-done.6), kind=kOutput, calls=%fused_computation.15 | convolution fusion | flops 605552640 | bytes 6684672 | tf_op jit(solution)/shard_map/dot_general | solution.py:41
  75.0 1.9 %fusion.6 = f32[512,3712]{1,0:T(8,128)} fusion(f32[512,3712]{1,0:T(8,128)} %add_dynamic-update-slice_fusion, f32[512,640]{1,0:T(8,128)S(1)} %copy-done.10, bf16[640,640]{1,0:T(8,128)(2,1)S(1)} %copy-done.15, f32[512,640]{1,0:T(8,128)S(1)} %copy-done.3, bf16[512,3712]{1,0:T(8,128)(2,1)S(1)} %copy-done.6), kind=kOutput, calls=%fused_computation.22 | convolution fusion | flops 420741120 | bytes 5406720 | tf_op jit(solution)/shard_map/dot_general | solution.py:41
  77.0 1.9 %fusion.5 = f32[512,3712]{1,0:T(8,128)} fusion(f32[512,3712]{1,0:T(8,128)} %fusion.6, f32[512,640]{1,0:T(8,128)S(1)} %copy-done.9, bf16[640,640]{1,0:T(8,128)(2,1)S(1)} %copy-done.17, f32[512,640]{1,0:T(8,128)S(1)} %copy-done.3, bf16[512,3712]{1,0:T(8,128)(2,1)S(1)} %copy-done.6), kind=kOutput, calls=%fused_computation.20 | convolution fusion | flops 420741120 | bytes 5406720 | tf_op jit(solution)/shard_map/dot_general | solution.py:41
  78.9 7.3 %fusion.3 = f32[32,3712]{1,0:T(8,128)} fusion(f32[512,3712]{1,0:T(8,128)} %fusion.5, f32[512,3712]{1,0:T(8,128)S(1)} %bitcast.114, s32[512]{0:T(512)S(1)} %bitcast.127, pred[512]{0:T(512)(128)(4,1)S(1)} %compare_reduce_fusion), kind=kOutput, calls=%fused_computation.11 | convolution fusion | flops 731742208 | bytes 15682048 | tf_op jit(solution)/shard_map/dot_general | solution.py:45
  86.2 1.6 %gather_fusion = bf16[29,128,128]{2,1,0:T(8,128)(2,1)} fusion(bf16[7,128,128]{2,1,0:T(8,128)(2,1)S(1)} %copy-done.13, s32[1024]{0:T(1024)S(1)} %pad_clamp_fusion.1), kind=kCustom, calls=%fused_computation | custom fusion | bytes 1900660 | tf_op jit(solution)/shard_map/gather | solution.py:141
  87.8 0.1 copy.55
  87.9 8.1 %all-gather.3 = f32[4,32,8]{1,2,0:T(8,128)S(1)} all-gather(f32[1,32,8]{1,2,0:T(8,128)S(1)} %copy.55), channel_id=2, replica_groups=mesh['dst'=8,'src'=4] {'src'}, dimensions={0}, use_global_device_ids=true | all-gather | bytes 5120 | tf_op jit(solution)/shard_map/all_gather | solution.py:30
  95.9 0.1 convolution_bitcast_fusion
  96.1 8.4 %all-gather.4 = f32[4,32,8]{1,2,0:T(8,128)S(1)} all-gather(f32[1,32,8]{1,2,0:T(8,128)S(1)} %convolution_bitcast_fusion), channel_id=3, replica_groups=mesh['dst'=8,'src'=4] {'src'}, dimensions={0}, use_global_device_ids=true | all-gather | bytes 5120 | tf_op jit(solution)/shard_map/all_gather | solution.py:30
  104.4 16.6 %all-gather.7.cloned.1.call-done = f32[128,3712]{1,0:T(8,128)} async-done(((f32[32,3712]{1,0:T(8,128)}), f32[128,3712]{1,0:T(8,128)}) %all-gather.7.cloned.1.call-update) | async-done | bytes 1900560 | tf_op jit(solution)/shard_map/all_gather | solution.py:30
  121.0 1.1 slice.44
  122.1 5.9 %while.19 = (s32[]{:T(128)}, f32[32,8]{0,1:T(8,128)S(1)}, f32[32,8]{0,1:T(8,128)S(1)}, f32[32,3712]{1,0:T(8,128)S(1)}, f32[4,32,8]{1,2,0:T(8,128)S(1)}, /*index=...) while((s32[]{:T(128)}, f32[32,8]{0,1:T(8,128)S(1)}, ...), condition=%wide.region_3.4_spmd, body=%wide.region_2.3_spmd.sunk | while | flops 357893 | bytes 3467415 | solution.py:35
  122.2 0.1 copy.75
  122.2 0.1 tile.121
  122.3 0.1 copy.76
  122.3 0.1 tile.122
  122.4 1.7 %fusion.50 = f32[32,3712]{1,0:T(8,128)S(1)} fusion(f32[4,8,29,128]{3,2,1,0:T(8,128)S(1)} %bitcast.111, f32[32,3712]{1,0:T(8,128)S(1)} %get-tuple-element.274, f32[4,8,29,128]{3,2,1,0:T(8,128)S(1)} %bitcast.112, f32[4,32,3712]{2,1,0:T(8,128)} %get-tuple-element.287, s32[]{:T(128)S(6)} %select_n.194), kind=kLoop, calls=%fused_computation.3.clone.1 | loop fusion | flops 356352 | bytes 2375684 | tf_op jit(solution)/shard_map/while/body/eval_jaxpr/add | solution.py:129
  124.1 0.1 copy.75
  124.3 0.1 copy.76
  124.3 0.1 tile.122
  124.4 1.7 %fusion.50 = f32[32,3712]{1,0:T(8,128)S(1)} fusion(f32[4,8,29,128]{3,2,1,0:T(8,128)S(1)} %bitcast.111, f32[32,3712]{1,0:T(8,128)S(1)} %get-tuple-element.274, f32[4,8,29,128]{3,2,1,0:T(8,128)S(1)} %bitcast.112, f32[4,32,3712]{2,1,0:T(8,128)} %get-tuple-element.287, s32[]{:T(128)S(6)} %select_n.194), kind=kLoop, calls=%fused_computation.3.clone.1 | loop fusion | flops 356352 | bytes 2375684 | tf_op jit(solution)/shard_map/while/body/eval_jaxpr/add | solution.py:129
  126.1 0.1 copy.75
  126.2 0.1 copy.76
  126.4 1.7 %fusion.50 = f32[32,3712]{1,0:T(8,128)S(1)} fusion(f32[4,8,29,128]{3,2,1,0:T(8,128)S(1)} %bitcast.111, f32[32,3712]{1,0:T(8,128)S(1)} %get-tuple-element.274, f32[4,8,29,128]{3,2,1,0:T(8,128)S(1)} %bitcast.112, f32[4,32,3712]{2,1,0:T(8,128)} %get-tuple-element.287, s32[]{:T(128)S(6)} %select_n.194), kind=kLoop, calls=%fused_computation.3.clone.1 | loop fusion | flops 356352 | bytes 2375684 | tf_op jit(solution)/shard_map/while/body/eval_jaxpr/add | solution.py:129
  128.0 0.1 constant_dynamic-slice_fusion
  128.1 0.1 copy.63
  128.2 0.1 broadcast_in_dim.95
  128.3 0.1 tile.112
  128.3 2.2 %fusion.7 = bf16[8,3712]{1,0:T(8,128)(2,1)} fusion(bf16[29,128,128]{2,1,0:T(8,128)(2,1)} %gather_fusion, f32[32,3712]{1,0:T(8,128)S(1)} %get-tuple-element.182, s32[]{:T(128)S(6)} %select_n.144, f32[8,128]{1,0:T(8,128)S(1)} %tile.112), kind=kOutput, calls=%fused_computation.26 | convolution fusion | flops 7691264 | bytes 1132548 | tf_op jit(solution)/shard_map/acx,cxy->acy/dot_general | solution.py:142
  (79 shorter events, 0.5 us)
Async XLA Ops:
  6.5 33.8 %copy-start = (bf16[896,896]{1,0:T(8,128)(2,1)S(1)}, bf16[896,896]{1,0:T(8,128)(2,1)}, u32[]{:S(2)}) copy-start(bf16[896,896]{1,0:T(8,128)(2,1)} %param.25) | copy-start | bytes 4816900
  6.5 114.5 %all-gather.7.cloned.1.call-start = ((), (), s32[]{:S(2)}) async-start(), calls=%async_computation | async-start | bytes 2375680 | tf_op jit(solution)/shard_map/all_gather | solution.py:30
  6.5 3.7 %collective-permute-start = (bf16[1,8,3712]{2,1,0:T(8,128)(2,1)}, bf16[1,8,3712]{2,1,0:T(8,128)(2,1)S(1)}, u32[]{:S(2)}, u32[]{:S(2)}) collective-permute-start(bf16[1,8,3712]{2,1,0:T(8,128)(2,1)} %bitcast.124), channel_id=1, source_target_pairs={{0,4},{4,0},{8,12},{12,8},{16,20},{20,16},{24,28},{28,24},{1,5},{5... | collective-permute-start | bytes 178184 | tf_op jit(solution)/shard_map/ppermute | solution.py:22
  11.1 6.5 %collective-permute-start.1 = (bf16[2,8,3712]{2,1,0:T(8,128)(2,1)S(1)}, bf16[2,8,3712]{2,1,0:T(8,128)(2,1)S(1)}, u32[]{:S(2)}, u32[]{:S(2)}) collective-permute-start(bf16[2,8,3712]{2,1,0:T(8,128)(2,1)S(1)} %pad_maximum_fusion.1), channel_id=1, source_target_pairs={{0,8},{4,12},{8,0},{12,4},{16,24},{20,28},{24,16},{28,20},{1,9},{5... | collective-permute-start | bytes 356360 | tf_op jit(solution)/shard_map/ppermute | solution.py:22
  17.7 3.5 %copy-start.18 = (bf16[2,8,3712]{2,1,0:T(8,128)(2,1)}, bf16[2,8,3712]{2,1,0:T(8,128)(2,1)S(1)}, u32[]{:S(2)}) copy-start(bf16[2,8,3712]{2,1,0:T(8,128)(2,1)S(1)} %get-tuple-element.204) | copy-start | bytes 356356
  17.7 3.5 %copy-start.20 = (bf16[2,8,3712]{2,1,0:T(8,128)(2,1)}, bf16[2,8,3712]{2,1,0:T(8,128)(2,1)S(1)}, u32[]{:S(2)}) copy-start(bf16[2,8,3712]{2,1,0:T(8,128)(2,1)S(1)} %get-tuple-element.205) | copy-start | bytes 356356
  18.5 13.8 %collective-permute-start.2 = (bf16[4,8,3712]{2,1,0:T(8,128)(2,1)}, bf16[4,8,3712]{2,1,0:T(8,128)(2,1)}, u32[]{:S(2)}, u32[]{:S(2)}) collective-permute-start(bf16[4,8,3712]{2,1,0:T(8,128)(2,1)} %pad_maximum_fusion), channel_id=1, source_target_pairs={{0,16},{4,20},{8,24},{12,28},{16,0},{20,4},{24,8},{28,12},{1,17},{... | collective-permute-start | bytes 712712 | tf_op jit(solution)/shard_map/ppermute | solution.py:22
  25.3 1.6 %copy-start.12 = (f32[512,128]{0,1:T(8,128)S(1)}, f32[512,128]{0,1:T(8,128)}, u32[]{:S(2)}) copy-start(f32[512,128]{0,1:T(8,128)} %fusion.13) | copy-start | bytes 786436
  27.1 5.2 %copy-start.19 = (bf16[2,8,3712]{2,1,0:T(8,128)(2,1)S(1)}, bf16[2,8,3712]{2,1,0:T(8,128)(2,1)}, u32[]{:S(2)}) copy-start(bf16[2,8,3712]{2,1,0:T(8,128)(2,1)} %copy-done.18) | copy-start | bytes 356356
  27.1 5.2 %copy-start.21 = (bf16[2,8,3712]{2,1,0:T(8,128)(2,1)S(1)}, bf16[2,8,3712]{2,1,0:T(8,128)(2,1)}, u32[]{:S(2)}) copy-start(bf16[2,8,3712]{2,1,0:T(8,128)(2,1)} %copy-done.20) | copy-start | bytes 356356
  37.6 2.7 %copy-start.7 = (f32[512,896]{1,0:T(8,128)S(1)}, f32[512,896]{1,0:T(8,128)}, u32[]{:S(2)}) copy-start(f32[512,896]{1,0:T(8,128)} %copy.53) | copy-start | bytes 5505028
  40.3 2.5 %copy-start.4 = (bf16[512,3712]{1,0:T(8,128)(2,1)}, bf16[512,3712]{1,0:T(8,128)(2,1)S(1)}, u32[]{:S(2)}) copy-start(bf16[512,3712]{1,0:T(8,128)(2,1)S(1)} %broadcast_select_fusion) | copy-start | bytes 11403268
  40.4 2.5 %copy-start.23 = (f32[128]{0:T(128)S(1)}, f32[128]{0:T(128)}, u32[]{:S(2)}) copy-start(f32[128]{0:T(128)} %param.30) | copy-start | bytes 1540
  40.4 4.4 %copy-start.22 = (f32[1,8,512]{2,1,0:T(8,128)S(1)}, f32[1,8,512]{2,1,0:T(8,128)}, u32[]{:S(2)}) copy-start(f32[1,8,512]{2,1,0:T(8,128)} %param.23) | copy-start | bytes 49156
  40.4 4.8 %copy-start.1 = (f32[512,768]{1,0:T(8,128)S(1)}, f32[512,768]{1,0:T(8,128)}, u32[]{:S(2)}) copy-start(f32[512,768]{1,0:T(8,128)} %copy.57) | copy-start | bytes 4718596
  45.2 3.7 %copy-start.5 = (bf16[512,3712]{1,0:T(8,128)(2,1)S(1)}, bf16[512,3712]{1,0:T(8,128)(2,1)}, u32[]{:S(2)}) copy-start(bf16[512,3712]{1,0:T(8,128)(2,1)} %copy-done.4) | copy-start | bytes 11403268
  45.2 3.7 %copy-start.11 = (bf16[768,768]{1,0:T(8,128)(2,1)S(1)}, bf16[768,768]{1,0:T(8,128)(2,1)}, u32[]{:S(2)}) copy-start(bf16[768,768]{1,0:T(8,128)(2,1)} %param.27) | copy-start | bytes 3538948
  48.9 2.0 %copy-start.2 = (f32[512,640]{1,0:T(8,128)S(1)}, f32[512,640]{1,0:T(8,128)}, u32[]{:S(2)}) copy-start(f32[512,640]{1,0:T(8,128)} %copy.60) | copy-start | bytes 3932164
  48.9 2.0 %copy-start.16 = (bf16[640,640]{1,0:T(8,128)(2,1)S(1)}, bf16[640,640]{1,0:T(8,128)(2,1)}, u32[]{:S(2)}) copy-start(bf16[640,640]{1,0:T(8,128)(2,1)} %param.28) | copy-start | bytes 2457604
  50.9 1.9 %copy-start.14 = (bf16[640,640]{1,0:T(8,128)(2,1)S(1)}, bf16[640,640]{1,0:T(8,128)(2,1)}, u32[]{:S(2)}) copy-start(bf16[640,640]{1,0:T(8,128)(2,1)} %param.29) | copy-start | bytes 2457604
  67.4 4.2 %copy-start.6 = (bf16[512,3712]{1,0:T(8,128)(2,1)S(1)}, bf16[512,3712]{1,0:T(8,128)(2,1)}, u32[]{:S(2)}) copy-start(bf16[512,3712]{1,0:T(8,128)(2,1)} %copy-done.4) | copy-start | bytes 11403268
  67.4 4.2 %copy-start.8 = (f32[512,768]{1,0:T(8,128)S(1)}, f32[512,768]{1,0:T(8,128)}, u32[]{:S(2)}) copy-start(f32[512,768]{1,0:T(8,128)} %fusion.31) | copy-start | bytes 4718596
  67.4 7.6 %copy-start.10 = (f32[512,640]{1,0:T(8,128)S(1)}, f32[512,640]{1,0:T(8,128)}, u32[]{:S(2)}) copy-start(f32[512,640]{1,0:T(8,128)} %fusion.30) | copy-start | bytes 3932164
  71.6 3.4 %copy-start.3 = (f32[512,640]{1,0:T(8,128)S(1)}, f32[512,640]{1,0:T(8,128)}, u32[]{:S(2)}) copy-start(f32[512,640]{1,0:T(8,128)} %copy.60) | copy-start | bytes 3932164
  71.6 3.4 %copy-start.15 = (bf16[640,640]{1,0:T(8,128)(2,1)S(1)}, bf16[640,640]{1,0:T(8,128)(2,1)}, u32[]{:S(2)}) copy-start(bf16[640,640]{1,0:T(8,128)(2,1)} %param.29) | copy-start | bytes 2457604
  71.6 5.4 %copy-start.17 = (bf16[640,640]{1,0:T(8,128)(2,1)S(1)}, bf16[640,640]{1,0:T(8,128)(2,1)}, u32[]{:S(2)}) copy-start(bf16[640,640]{1,0:T(8,128)(2,1)} %param.28) | copy-start | bytes 2457604
  71.6 7.2 %slice-start = ((s8[7602176]{0:T(1024)(128)(4,1)}), s8[4194304]{0:T(1024)(128)(4,1)S(1)}, s32[]{:S(2)}) async-start(s8[7602176]{0:T(1024)(128)(4,1)} %bitcast.113), calls=%async_computation.1 | async-start | bytes 8388608
  75.0 2.0 %copy-start.9 = (f32[512,640]{1,0:T(8,128)S(1)}, f32[512,640]{1,0:T(8,128)}, u32[]{:S(2)}) copy-start(f32[512,640]{1,0:T(8,128)} %fusion.29) | copy-start | bytes 3932164
  75.0 3.8 %slice-start.1 = ((s8[7602176]{0:T(1024)(128)(4,1)}), s8[3407872]{0:T(1024)(128)(4,1)S(1)}, s32[]{:S(2)}) async-start(s8[7602176]{0:T(1024)(128)(4,1)} %bitcast.113), calls=%async_computation.2 | async-start | bytes 6815744
  78.9 7.3 %copy-start.24 = (s32[29]{0:T(128)S(1)}, s32[29]{0:T(128)}, u32[]{:S(2)}) copy-start(s32[29]{0:T(128)} %constant.138) | copy-start | bytes 352
  78.9 7.3 %copy-start.13 = (bf16[7,128,128]{2,1,0:T(8,128)(2,1)S(1)}, bf16[7,128,128]{2,1,0:T(8,128)(2,1)}, u32[]{:S(2)}) copy-start(bf16[7,128,128]{2,1,0:T(8,128)(2,1)} %param.31) | copy-start | bytes 688132
Sparse Core Ops, SparseCore 0:
  86.3 34.7 all-gather.6
